TPU v7x, 256 devices: a whole 4x4x8 slice. The times are simulated.
256 devices in a mesh: grp: 4 (over z_hi), dev: 64 (over x, z_lo, y, core).
Axes of the slice: x: 4, y: 4, z: 8 (z_hi: 4, z_lo: 2; z = z_hi * 2 + z_lo), core: 2. Of those that a mesh axis runs over, the one named last changes fastest.
Arguments:
- images: bfloat16 [12288, 1536], P(('grp', 'dev')), may hold values from -1 to 1, as said below
- texts: bfloat16 [12288, 1536], P(('grp', 'dev')), may hold values from -1 to 1, as said below
- logit_scale: float32 [1], replicated, may hold values from 20 to 60
- logit_bias: float32 [1], replicated, may hold values from -12 to -8
Outputs:
- grad_image: float32 [12288, 1536], P(('grp', 'dev'))
- grad_text: float32 [12288, 1536], P(('grp', 'dev'))
- loss: float32 [1], replicated
Inputs may be any that keep to these rules, and one draw needn't show every extreme that they name: `images`: every row has length 1 up to bfloat16 rounding. `texts`: every row has length 1 up to bfloat16 rounding.
All inputs are finite; a program needn't handle non-finite values.
Results may differ from a plain program's by a relative error of at most 0.00095.
Values may be sent and summed in bfloat16 or wider, within the bound.
No kernel may reach another device: no remote copies, remote signals or barrier semaphores. Data moves between devices by JAX's collectives and lax.ppermute only.
A program may use at most 128 MiB of HBM per device.

v0:
```python
import functools

import jax
import jax.numpy as jnp
from jax import lax
from jax.sharding import Mesh
from jax.sharding import PartitionSpec as P

DEV = ("dev_0", "dev_1", "dev_2", "dev_3")
GRP_DEV = ("grp", "dev_0", "dev_1", "dev_2", "dev_3")


def from_everyone(x, axis):
    size = lax.axis_size(axis)
    return lax.all_to_all(jnp.broadcast_to(x[None], (size, *x.shape)), axis, 0, 0, tiled=True)


def joined_along(tiles, dim):
    tiles = jnp.moveaxis(tiles, 0, dim)
    dims = tiles.shape
    return tiles.reshape(*dims[:dim], dims[dim] * dims[dim + 1], *dims[dim + 2 :])


def collect(x, axis, dim):
    tiles = from_everyone(x, axis)
    return joined_along(tiles, dim)


def split_up(x, dim, size):
    dims = x.shape
    tiles = x.reshape(*dims[:dim], size, dims[dim] // size, *dims[dim + 1 :])
    return jnp.moveaxis(tiles, dim, 0)


def sent_and_summed(x, axis, dim):
    tiles = split_up(x, dim, lax.axis_size(axis))
    arrived = lax.all_to_all(tiles, axis, split_axis=0, concat_axis=0, tiled=True)
    return arrived.sum(axis=0)


def over_axes(x, axes):
    return functools.reduce(lax.psum, axes, x)


def pair_logits(left_rows, left_ids, shard_rows, shard_ids, multiplier, offset):
    logits = (
        lax.dot_general(
            left_rows, shard_rows, (((1,), (1,)), ((), ())), preferred_element_type=jnp.float32
        )
        * multiplier
        + offset
    )
    matched = left_ids[:, None] == shard_ids[None, :]
    return (logits, matched)


def pair_weights(logits, matched):
    return (jax.nn.sigmoid(logits) - matched.astype(jnp.float32)).astype(jnp.bfloat16)


def pair_loss(logits, matched):
    labels = jnp.where(matched, 1.0, -1.0).astype(jnp.float32)
    return -jnp.sum(jax.nn.log_sigmoid(labels * logits))


def shards(images, texts, logit_scale, logit_bias):
    own_rows = images.shape[0]
    group_size = lax.axis_size(DEV)
    groups = lax.axis_size("grp")
    group_index = lax.axis_index("grp")
    member = lax.axis_index(DEV)
    multiplier = logit_scale[0]
    offset = logit_bias[0]
    slab_start = group_index * group_size * own_rows
    local_iota = jnp.arange(groups * own_rows, dtype=jnp.int32)
    spread_ids = (
        local_iota // own_rows * group_size * own_rows + member * own_rows + local_iota % own_rows
    )
    image_all = collect(images, "grp", 0)
    shard_rows = lax.all_gather(texts, DEV, axis=0, tiled=True)
    shard_ids = slab_start + jnp.arange(shard_rows.shape[0], dtype=jnp.int32)
    logits, matched = pair_logits(image_all, spread_ids, shard_rows, shard_ids, multiplier, offset)
    weights = pair_weights(logits, matched)
    grad_sum = jnp.dot(weights, shard_rows, preferred_element_type=jnp.float32)
    grad_sum, loss_sum = (grad_sum, pair_loss(logits, matched))
    text_all = collect(texts, "grp", 0)
    shard_rows = lax.all_gather(images, DEV, axis=0, tiled=True)
    shard_ids = slab_start + jnp.arange(shard_rows.shape[0], dtype=jnp.int32)
    logits, matched = pair_logits(text_all, spread_ids, shard_rows, shard_ids, multiplier, offset)
    weights = pair_weights(logits, matched)
    grad_back = jnp.dot(weights, shard_rows, preferred_element_type=jnp.float32)
    grad_text = sent_and_summed(multiplier * grad_back, "grp", 0)
    grad_image = sent_and_summed(multiplier * grad_sum, "grp", 0)
    loss_total = over_axes(loss_sum, GRP_DEV)
    batch_all = own_rows * group_size * groups
    return (grad_image, grad_text, (loss_total / batch_all).reshape(1))


def solution(mesh):
    split = Mesh(
        mesh.devices.reshape(mesh.shape["grp"], 4, 2, 4, 2),
        ("grp", "dev_0", "dev_1", "dev_2", "dev_3"),
    )
    in_specs = (P(GRP_DEV, None), P(GRP_DEV, None), P(), P())
    out_specs = (P(GRP_DEV, None), P(GRP_DEV, None), P())
    return jax.shard_map(
        shards, mesh=split, in_specs=in_specs, out_specs=out_specs, check_vma=False
    )
```

profile of v0, /device:TPU:28, one launch (start us, length us, event | category | flops | bytes accessed | tf_op | source)
XLA Modules:
  0.0 346.1 jit_solution(8935938616538621625)
XLA Ops:
  7.2 0.0 all-gather.3.cloned.1.call-start
  7.2 0.7 all-gather.3.cloned.1.call-update
  7.9 0.0 all-gather.5.cloned.1.call-start
  8.0 0.7 all-gather.5.cloned.1.call-update
  8.7 1.8 broadcast_in_dim.10
  10.4 8.5 %all-to-all-start = ((bf16[4,48,1536]{2,1,0:T(8,128)(2,1)}), bf16[4,48,1536]{2,1,0:T(8,128)(2,1)S(1)}, u32[]{:S(2)}, u32[]{:S(2)}) async-start(bf16[4,48,1536]{2,1,0:T(8,128)(2,1)} %broadcast_in_dim.10), calls=%async_computation | async-start | bytes 1179648 | tf_op jit(solution)/shard_map/all_to_all | solution.py:15
  20.2 15.2 %all-to-all-done = bf16[4,48,1536]{2,1,0:T(8,128)(2,1)S(1)} async-done(((bf16[4,48,1536]{2,1,0:T(8,128)(2,1)}), bf16[4,48,1536]{2,1,0:T(8,128)(2,1)S(1)}, u32[]{:S(2)}, u32[]{:S(2)}) %all-to-all-start) | async-done | bytes 589856 | tf_op jit(solution)/shard_map/all_to_all | solution.py:15
  35.5 0.9 broadcast_in_dim.11
  36.3 4.1 %all-to-all-start.2 = ((bf16[4,48,1536]{2,1,0:T(8,128)(2,1)}), bf16[4,48,1536]{2,1,0:T(8,128)(2,1)S(1)}, u32[]{:S(2)}, u32[]{:S(2)}) async-start(bf16[4,48,1536]{2,1,0:T(8,128)(2,1)} %broadcast_in_dim.11), calls=%async_computation.2 | async-start | bytes 1179648 | tf_op jit(solution)/shard_map/all_to_all | solution.py:15
  40.5 89.7 %all-gather.3.cloned.1.call-done = bf16[3072,1536]{1,0:T(8,128)(2,1)} async-done(((bf16[48,1536]{1,0:T(8,128)(2,1)}), bf16[3072,1536]{1,0:T(8,128)(2,1)}) %all-gather.3.cloned.1.call-update) | async-done | bytes 9437200 | tf_op jit(solution)/shard_map/all_gather | solution.py:80
  130.2 8.7 %fusion.11 = (f32[]{:T(128)}, f32[192,3072]{1,0:T(8,128)S(1)}) fusion(s32[3072]{0:T(1024)S(1)} %iota_add_fusion, s32[192]{0:T(256)S(1)} %fusion.18, f32[]{:T(128)} %bitcast.16, f32[]{:T(128)} %bitcast.14, bf16[192,1536]{1,0:T(8,128)(2,1)S(1)} %bitcast.18, bf16[3072,1536]{1,0:T(8,128)(2,1)} %all-gather.3.cloned.1.call-done), kind=kOutput, calls=%fused_computation.18 | convolution fusion | flops 1819607040 | bytes 12399372 | tf_op jit(solution)/shard_map/dot_general | solution.py:47
  139.0 3.1 convolution_multiply_fusion.3
  142.0 0.0 all-to-all-done.2
  142.0 6.3 %all-to-all-start.1 = ((f32[4,48,1536]{2,1,0:T(8,128)}), f32[4,48,1536]{2,1,0:T(8,128)S(1)}, u32[]{:S(2)}, u32[]{:S(2)}) async-start(f32[4,48,1536]{2,1,0:T(8,128)} %bitcast.3), calls=%async_computation.1 | async-start | bytes 2359296 | tf_op jit(solution)/shard_map/all_to_all | solution.py:37
  148.4 107.9 %all-gather.5.cloned.1.call-done = bf16[3072,1536]{1,0:T(8,128)(2,1)} async-done(((bf16[48,1536]{1,0:T(8,128)(2,1)}), bf16[3072,1536]{1,0:T(8,128)(2,1)}) %all-gather.5.cloned.1.call-update) | async-done | bytes 9437200 | tf_op jit(solution)/shard_map/all_gather | solution.py:87
  256.3 12.5 %convolution_multiply_fusion.2 = f32[192,1536]{1,0:T(8,128)} fusion(bf16[3072,1536]{1,0:T(8,128)(2,1)} %all-gather.5.cloned.1.call-done, bf16[192,1536]{1,0:T(8,128)(2,1)S(1)} %bitcast.19, s32[3072]{0:T(1024)S(1)} %iota_add_fusion, f32[]{:T(128)} %bitcast.17, f32[]{:T(128)} %bitcast.15, s32[192]{0:T(256)S(1)} %fusion.18), kind=kOutput, calls=%fused_computation.13 | convolution fusion | flops 3629481984 | bytes 11219720 | tf_op jit(solution)/shard_map/dot_general | solution.py:91
  268.8 6.7 %all-to-all-start.3 = ((f32[4,48,1536]{2,1,0:T(8,128)}), f32[4,48,1536]{2,1,0:T(8,128)S(1)}, u32[]{:S(2)}, u32[]{:S(2)}) async-start(f32[4,48,1536]{2,1,0:T(8,128)} %bitcast.5), calls=%async_computation.3 | async-start | bytes 2359296 | tf_op jit(solution)/shard_map/all_to_all | solution.py:37
  275.6 34.1 %psum.35 = f32[]{:T(128)} all-reduce(f32[]{:T(128)} %get-tuple-element.3), channel_id=1, replica_groups=mesh['grp'=4,'dev_0'=4,'dev_1'=2,'dev_2'=4,'dev_3'=2] {'grp'}, use_global_device_ids=true, to_apply=%region_3.4 | all-reduce | flops 1 | bytes 8 | tf_op jit(solution)/shard_map/psum | solution.py:42
  309.6 7.9 %psum.36 = f32[]{:T(128)} all-reduce(f32[]{:T(128)} %psum.35), channel_id=1, replica_groups=mesh['grp'=4,'dev_0'=4,'dev_1'=2,'dev_2'=4,'dev_3'=2] {'dev_0'}, use_global_device_ids=true, to_apply=%region_4.5 | all-reduce | flops 1 | bytes 8 | tf_op jit(solution)/shard_map/psum | solution.py:42
  317.5 6.0 %psum.37 = f32[]{:T(128)} all-reduce(f32[]{:T(128)} %psum.36), channel_id=1, replica_groups=mesh['grp'=4,'dev_0'=4,'dev_1'=2,'dev_2'=4,'dev_3'=2] {'dev_1'}, use_global_device_ids=true, to_apply=%region_5.6 | all-reduce | flops 1 | bytes 8 | tf_op jit(solution)/shard_map/psum | solution.py:42
  323.5 9.2 %psum.38 = f32[]{:T(128)} all-reduce(f32[]{:T(128)} %psum.37), channel_id=1, replica_groups=mesh['grp'=4,'dev_0'=4,'dev_1'=2,'dev_2'=4,'dev_3'=2] {'dev_2'}, use_global_device_ids=true, to_apply=%region_6.7 | all-reduce | flops 1 | bytes 8 | tf_op jit(solution)/shard_map/psum | solution.py:42
  332.8 3.1 psum.39
  336.5 0.8 reduce_sum.27
  337.3 0.8 reduce_sum.28
  (8 shorter events, 0.0 us)
Async XLA Ops:
  7.2 28.3 %copy-start = (bf16[48,1536]{1,0:T(8,128)(2,1)S(1)}, bf16[48,1536]{1,0:T(8,128)(2,1)}, u32[]{:S(2)}) copy-start(bf16[48,1536]{1,0:T(8,128)(2,1)} %param.5) | copy-start | bytes 442372
  7.2 123.0 %all-gather.3.cloned.1.call-start = ((), (), s32[]{:S(2)}) async-start(), calls=%async_computation.4 | async-start | bytes 9584640 | tf_op jit(solution)/shard_map/all_gather | solution.py:80
  7.9 248.4 %all-gather.5.cloned.1.call-start = ((), (), s32[]{:S(2)}) async-start(), calls=%async_computation.5 | async-start | bytes 9584640 | tf_op jit(solution)/shard_map/all_gather | solution.py:87
  10.4 25.0 %all-to-all-start = ((bf16[4,48,1536]{2,1,0:T(8,128)(2,1)}), bf16[4,48,1536]{2,1,0:T(8,128)(2,1)S(1)}, u32[]{:S(2)}, u32[]{:S(2)}) async-start(bf16[4,48,1536]{2,1,0:T(8,128)(2,1)} %broadcast_in_dim.10), calls=%async_computation | async-start | bytes 1179648 | tf_op jit(solution)/shard_map/all_to_all | solution.py:15
  36.3 105.7 %all-to-all-start.2 = ((bf16[4,48,1536]{2,1,0:T(8,128)(2,1)}), bf16[4,48,1536]{2,1,0:T(8,128)(2,1)S(1)}, u32[]{:S(2)}, u32[]{:S(2)}) async-start(bf16[4,48,1536]{2,1,0:T(8,128)(2,1)} %broadcast_in_dim.11), calls=%async_computation.2 | async-start | bytes 1179648 | tf_op jit(solution)/shard_map/all_to_all | solution.py:15
  130.2 8.7 %copy-start.1 = (bf16[3072,1536]{1,0:T(8,128)(2,1)S(1)}, bf16[3072,1536]{1,0:T(8,128)(2,1)}, u32[]{:S(2)}) copy-start(bf16[3072,1536]{1,0:T(8,128)(2,1)} %all-gather.3.cloned.1.call-done) | copy-start | bytes 28311556
  142.0 126.8 %all-to-all-start.1 = ((f32[4,48,1536]{2,1,0:T(8,128)}), f32[4,48,1536]{2,1,0:T(8,128)S(1)}, u32[]{:S(2)}, u32[]{:S(2)}) async-start(f32[4,48,1536]{2,1,0:T(8,128)} %bitcast.3), calls=%async_computation.1 | async-start | bytes 2359296 | tf_op jit(solution)/shard_map/all_to_all | solution.py:37
  268.8 68.5 %all-to-all-start.3 = ((f32[4,48,1536]{2,1,0:T(8,128)}), f32[4,48,1536]{2,1,0:T(8,128)S(1)}, u32[]{:S(2)}, u32[]{:S(2)}) async-start(f32[4,48,1536]{2,1,0:T(8,128)} %bitcast.5), calls=%async_computation.3 | async-start | bytes 2359296 | tf_op jit(solution)/shard_map/all_to_all | solution.py:37
Sparse Core Ops, SparseCore 0:
  9.8 120.3 all-gather.2
  132.1 124.1 all-gather.4
where the time goes:
time: 352 us; the launch traced here: 346 us
  waiting for transfers between devices  214 us (61%)
  blocking collectives  60.3 us (17%)
  starting transfers between devices  25.7 us (7%)
  matrix products  24.4 us (7%)
  between operations  17.2 us (5%)
    all_gather x1, waiting for transfers between devices, shards(): shard_rows = lax.all_gather(images, DEV, axis=0, tiled=True)  108 us
    all_gather x1, waiting for transfers between devices, shards(): shard_rows = lax.all_gather(texts, DEV, axis=0, tiled=True)  89.7 us
    psum x5, blocking collectives, over_axes(): return functools.reduce(lax.psum, axes, x)  60.3 us
    all_to_all x2, waiting for transfers between devices, from_everyone(): lax.all_to_all(jnp.broadcast_to(x[None], (size, *x.shape)), axis, 0, 0, t...  15.2 us
    all_to_all x2, starting transfers between devices, sent_and_summed(): lax.all_to_all(tiles, axis, split_axis=0, concat_axis=0, tiled=True)  13 us
    all_to_all x2, starting transfers between devices, from_everyone(): lax.all_to_all(jnp.broadcast_to(x[None], (size, *x.shape)), axis, 0, 0, t...  12.6 us
    dot_general x1, matrix products, shards(): grad_back = jnp.dot(weights, shard_rows, preferred_element_type=jnp.float32)  12.5 us
    dot_general x1, matrix products, pair_logits(): lax.dot_general(left_rows, shard_rows, (((1,), (1,)), ((), ())), preferre...  8.74 us
  transfers between devices with their start and end apart: 6, of which 3 were waited for; matrix products, arithmetic and copies ran while one was open for 8% of the time, Pallas kernels for 0%

commit v1 on v0

v1 whole, which is shorter than its diff:
```python
import jax
import jax.numpy as jnp
from jax import lax
from jax.sharding import Mesh
from jax.sharding import PartitionSpec as P

AXES = ("zh", "x", "zl", "y", "c")
PLANE = ("x", "y")
COLUMN = ("zh", "zl", "c")


def from_everyone(x, axes):
    size = lax.axis_size(axes)
    tiles = lax.all_to_all(jnp.broadcast_to(x[None], (size, *x.shape)), axes, 0, 0, tiled=True)
    return tiles.reshape(size * x.shape[0], *x.shape[1:])


def sent_and_summed(x, axes):
    size = lax.axis_size(axes)
    tiles = x.reshape(size, x.shape[0] // size, *x.shape[1:])
    return lax.all_to_all(tiles, axes, 0, 0, tiled=True).sum(axis=0)


def total(value, axes):
    size = lax.axis_size(axes)
    tile = jnp.broadcast_to(value, (size, 8, 128))
    return lax.all_to_all(tile, axes, 0, 0, tiled=True)[:, 0, 0].sum()


def shards(images, texts, logit_scale, logit_bias):
    rows = images.shape[0]
    multiplier = logit_scale[0]
    offset = logit_bias[0]
    left = from_everyone(images, PLANE)
    right = from_everyone(texts, COLUMN)
    logits = (
        lax.dot_general(left, right, (((1,), (1,)), ((), ())), preferred_element_type=jnp.float32)
        * multiplier
        + offset
    )
    left_ids = jnp.arange(left.shape[0], dtype=jnp.int32) - lax.axis_index(PLANE) * rows
    right_ids = jnp.arange(right.shape[0], dtype=jnp.int32) - lax.axis_index(COLUMN) * rows
    own = (left_ids >= 0) & (left_ids < rows)
    matched = (left_ids[:, None] == right_ids[None, :]) & own[:, None]
    weights = (jax.nn.sigmoid(logits) - matched.astype(jnp.float32)).astype(jnp.bfloat16)
    labels = jnp.where(matched, 1.0, -1.0).astype(jnp.float32)
    loss = -jnp.sum(jax.nn.log_sigmoid(labels * logits))
    grad_left = multiplier * jnp.dot(weights, right, preferred_element_type=jnp.float32)
    grad_right = multiplier * lax.dot_general(
        weights, left, (((0,), (0,)), ((), ())), preferred_element_type=jnp.float32
    )
    grad_image = sent_and_summed(grad_left, PLANE)
    grad_text = sent_and_summed(grad_right, COLUMN)
    loss = total(total(loss, PLANE), COLUMN)
    return (grad_image, grad_text, (loss / (rows * lax.axis_size(AXES))).reshape(1))


def solution(mesh):
    split = Mesh(mesh.devices.reshape(mesh.shape["grp"], 4, 2, 4, 2), AXES)
    in_specs = (P(AXES, None), P(AXES, None), P(), P())
    out_specs = (P(AXES, None), P(AXES, None), P())
    return jax.shard_map(
        shards, mesh=split, in_specs=in_specs, out_specs=out_specs, check_vma=False
    )
```

time: 352 us -> 332 us (0.943); the launches traced: 346 us -> 331 us
  blocking collectives: 60.3 us -> 45.8 us
  between operations: 17.2 us -> 3.79 us
  other arithmetic: 1.61 us -> 7.9 us
  waiting for transfers between devices: 214 us -> 220 us
  matrix products: 24.4 us -> 20.3 us
    all_to_all x4, waiting for transfers between devices: 15.3 us -> 220 us  [the longest x2 166 us: sent_and_summed(): return lax.all_to_all(tiles, axes, 0, 0, tiled=True).sum(axis=0)]
    all_gather x2 -> x0, waiting for transfers between devices: 198 us -> none  [the longest x1 108 us: shards(): shard_rows = lax.all_gather(images, DEV, axis=0, tiled=True)]
    psum x5 -> x0, blocking collectives: 60.3 us -> none  [over_axes(): return functools.reduce(lax.psum, axes, x)]
    all_to_all x0 -> x2, blocking collectives: none -> 45.8 us  [the longest x1 34.4 us: from_everyone(): lax.all_to_all(jnp.broadcast_to(x[None], (size, *x.shape)), axes, 0, 0, t...]
    reduce_sum x2 -> x4, other arithmetic: 1.6 us -> 7.88 us  [the longest x2 6.66 us: sent_and_summed(): return lax.all_to_all(tiles, axes, 0, 0, tiled=True).sum(axis=0)]
    dot_general x3, matrix products: 24.4 us -> 20.3 us  [the longest x1 7.07 us: shards(): jnp.dot(weights, right, preferred_element_type=jnp.float32)]
  transfers between devices with their start and end apart: 6 -> 4, of which waited for: 3 -> 4; matrix products, arithmetic and copies ran while one was open for 8% -> 5% of each run, Pallas kernels for 0% -> 0%
where the time goes in v1:
time: 332 us; the launch traced here: 331 us
  waiting for transfers between devices  220 us (66%)
  blocking collectives  45.8 us (14%)
  starting transfers between devices  28.7 us (9%)
  matrix products  20.3 us (6%)
  other arithmetic  7.9 us (2%)
  local copies, waits for them, and re-layouts  4.6 us (1%)
  between operations  3.79 us (1%)
    all_to_all x2, waiting for transfers between devices, sent_and_summed(): return lax.all_to_all(tiles, axes, 0, 0, tiled=True).sum(axis=0)  166 us
    all_to_all x1, waiting for transfers between devices, from_everyone(): lax.all_to_all(jnp.broadcast_to(x[None], (size, *x.shape)), axes, 0, 0, t...  53.7 us
    all_to_all x1, blocking collectives, from_everyone(): lax.all_to_all(jnp.broadcast_to(x[None], (size, *x.shape)), axes, 0, 0, t...  34.4 us
    all_to_all x2, starting transfers between devices, sent_and_summed(): return lax.all_to_all(tiles, axes, 0, 0, tiled=True).sum(axis=0)  15.5 us
    all_to_all x1, blocking collectives, total(): return lax.all_to_all(tile, axes, 0, 0, tiled=True)[:, 0, 0].sum()  11.3 us
    all_to_all x1, starting transfers between devices, from_everyone(): lax.all_to_all(jnp.broadcast_to(x[None], (size, *x.shape)), axes, 0, 0, t...  8.61 us
    dot_general x1, matrix products, shards(): jnp.dot(weights, right, preferred_element_type=jnp.float32)  7.07 us
    dot_general x1, matrix products, shards(): lax.dot_general(left, right, (((1,), (1,)), ((), ())), preferred_element_...  7.04 us
  transfers between devices with their start and end apart: 4, of which 4 were waited for; matrix products, arithmetic and copies ran while one was open for 5% of the time, Pallas kernels for 0%

profile of v1, /device:TPU:28, one launch (start us, length us, event | category | flops | bytes accessed | tf_op | source)
XLA Modules:
  0.0 331.4 jit_solution(17445278188339077998)
XLA Ops:
  0.6 1.1 broadcast_in_dim.12
  1.8 0.0 copy-start
  1.8 34.4 %all_to_all.30 = bf16[16,48,1536]{2,1,0:T(8,128)(2,1)S(1)} all-to-all(bf16[16,48,1536]{2,1,0:T(8,128)(2,1)S(1)} %broadcast_in_dim.12), channel_id=1, replica_groups=mesh['zh'=4,'x'=4,'zl'=2,'y'=4,'c'=2] {'x','y'}, dimensions={0} | all-to-all | bytes 4718592 | tf_op jit(solution)/shard_map/all_to_all | solution.py:14
  36.2 0.0 copy-done
  36.2 1.6 broadcast_in_dim.15
  37.8 8.6 %all-to-all-start.1 = ((bf16[16,48,1536]{2,1,0:T(8,128)(2,1)}), bf16[16,48,1536]{2,1,0:T(8,128)(2,1)}, u32[]{:S(2)}, u32[]{:S(2)}) async-start(bf16[16,48,1536]{2,1,0:T(8,128)(2,1)} %broadcast_in_dim.15), calls=%async_computation.1 | async-start | bytes 4718592 | tf_op jit(solution)/shard_map/all_to_all | solution.py:14
  47.8 53.7 %all-to-all-done.1 = bf16[16,48,1536]{2,1,0:T(8,128)(2,1)} async-done(((bf16[16,48,1536]{2,1,0:T(8,128)(2,1)}), bf16[16,48,1536]{2,1,0:T(8,128)(2,1)}, u32[]{:S(2)}, u32[]{:S(2)}) %all-to-all-start.1) | async-done | bytes 2359328 | tf_op jit(solution)/shard_map/all_to_all | solution.py:14
  101.5 7.0 %fusion = (f32[]{:T(128)}, f32[768,768]{1,0:T(8,128)}) fusion(s32[768]{0:T(1024)S(1)} %get-tuple-element.5, f32[]{:T(128)} %bitcast.15, f32[]{:T(128)} %bitcast.12, s32[768]{0:T(1024)S(1)} %get-tuple-element.6, pred[768]{0:T(1024)(128)(4,1)S(1)} %compare_and_fusion.1, bf16[768,1536]{1,0:T(8,128)(2,1)S(1)} %bitcast.19, bf16[768,1536]{1,0:T(8,128)(2,1)} %bitcast.2), kind=kOutput, calls=%fused_computation.3 | convolution fusion | flops 1820196864 | bytes 7084812 | tf_op jit(solution)/shard_map/dot_general | solution.py:37
  108.5 0.6 broadcast_in_dim.30
  109.2 11.3 %all_to_all.31 = f32[16,8,128]{2,1,0:T(8,128)S(1)} all-to-all(f32[16,8,128]{2,1,0:T(8,128)S(1)} %broadcast_in_dim.30), channel_id=1, replica_groups=mesh['zh'=4,'x'=4,'zl'=2,'y'=4,'c'=2] {'x','y'}, dimensions={0} | all-to-all | bytes 131072 | tf_op jit(solution)/shard_map/all_to_all | solution.py:27
  120.5 0.6 slice_reduce_fusion.1
  121.1 1.2 broadcast_in_dim.31
  122.3 4.6 %all-to-all-start.5 = ((f32[16,8,128]{2,1,0:T(8,128)}), f32[16,8,128]{2,1,0:T(8,128)S(1)}, u32[]{:S(2)}, u32[]{:S(2)}) async-start(f32[16,8,128]{2,1,0:T(8,128)} %broadcast_in_dim.31), calls=%async_computation.5 | async-start | bytes 131072 | tf_op jit(solution)/shard_map/all_to_all | solution.py:27
  126.9 7.1 %convolution_multiply_fusion.1 = f32[768,1536]{1,0:T(8,128)} fusion(bf16[768,1536]{1,0:T(8,128)(2,1)} %bitcast.2, f32[]{:T(128)} %bitcast.11, f32[768,768]{1,0:T(8,128)} %get-tuple-element.4, s32[768]{0:T(1024)S(1)} %get-tuple-element.5, f32[]{:T(128)} %bitcast.14, s32[768]{0:T(1024)S(1)} %get-tuple-element.6, pred[768]{0:T(1024)(128)(4,1)S(1)} %compare_and_fusion.1), kind=kOutput, calls=%fused_computation.2 | convolution fusion | flops 1819017216 | bytes 9444104 | tf_op jit(solution)/shard_map/dot_general | solution.py:48
  133.9 0.7 all-to-all-done.5
  134.7 8.1 %all-to-all-start.2 = ((f32[16,48,1536]{2,1,0:T(8,128)}), f32[16,48,1536]{2,1,0:T(8,128)}, u32[]{:S(2)}, u32[]{:S(2)}) async-start(f32[16,48,1536]{2,1,0:T(8,128)} %bitcast.18), calls=%async_computation.2 | async-start | bytes 9437184 | tf_op jit(solution)/shard_map/all_to_all | solution.py:21
  142.8 6.2 %convolution_multiply_fusion = f32[768,1536]{1,0:T(8,128)} fusion(bf16[768,1536]{1,0:T(8,128)(2,1)S(1)} %bitcast.20, f32[]{:T(128)} %bitcast.13, f32[768,768]{1,0:T(8,128)} %get-tuple-element.4, s32[768]{0:T(1024)S(1)} %get-tuple-element.5, f32[]{:T(128)} %bitcast.16, s32[768]{0:T(1024)S(1)} %get-tuple-element.6, pred[768]{0:T(1024)(128)(4,1)S(1)} %compare_and_fusion.1), kind=kOutput, calls=%fused_computation.1 | convolution fusion | flops 1819017216 | bytes 9444104 | tf_op jit(solution)/shard_map/dot_general | solution.py:49
  149.0 65.0 %all-to-all-done.2 = f32[16,48,1536]{2,1,0:T(8,128)} async-done(((f32[16,48,1536]{2,1,0:T(8,128)}), f32[16,48,1536]{2,1,0:T(8,128)}, u32[]{:S(2)}, u32[]{:S(2)}) %all-to-all-start.2) | async-done | bytes 4718624 | tf_op jit(solution)/shard_map/all_to_all | solution.py:21
  213.9 7.4 %all-to-all-start.3 = ((f32[16,48,1536]{2,1,0:T(8,128)}), f32[16,48,1536]{2,1,0:T(8,128)}, u32[]{:S(2)}, u32[]{:S(2)}) async-start(f32[16,48,1536]{2,1,0:T(8,128)} %bitcast.17), calls=%async_computation.3 | async-start | bytes 9437184 | tf_op jit(solution)/shard_map/all_to_all | solution.py:21
  221.4 0.6 slice_reduce_fusion
  222.6 3.3 %reduce_sum.45 = f32[48,1536]{1,0:T(8,128)} reduce(f32[16,48,1536]{2,1,0:T(8,128)} %all-to-all-done.2, f32[]{:T(128)} %constant.38.clone.1), dimensions={0}, to_apply=%region_0.1 | reduce | flops 1105920 | bytes 5013508 | tf_op jit(solution)/shard_map/reduce_sum | solution.py:21
  226.0 101.0 %all-to-all-done.3 = f32[16,48,1536]{2,1,0:T(8,128)} async-done(((f32[16,48,1536]{2,1,0:T(8,128)}), f32[16,48,1536]{2,1,0:T(8,128)}, u32[]{:S(2)}, u32[]{:S(2)}) %all-to-all-start.3) | async-done | bytes 4718624 | tf_op jit(solution)/shard_map/all_to_all | solution.py:21
  326.9 3.3 %reduce_sum.46 = f32[48,1536]{1,0:T(8,128)} reduce(f32[16,48,1536]{2,1,0:T(8,128)} %all-to-all-done.3, f32[]{:T(128)} %constant.38.clone.1), dimensions={0}, to_apply=%region_1.2 | reduce | flops 1105920 | bytes 5013508 | tf_op jit(solution)/shard_map/reduce_sum | solution.py:21
  (2 shorter events, 0.0 us)
Async XLA Ops:
  1.8 34.4 %copy-start = (bf16[48,1536]{1,0:T(8,128)(2,1)S(1)}, bf16[48,1536]{1,0:T(8,128)(2,1)}, u32[]{:S(2)}) copy-start(bf16[48,1536]{1,0:T(8,128)(2,1)} %param.5) | copy-start | bytes 442372
  37.8 63.6 %all-to-all-start.1 = ((bf16[16,48,1536]{2,1,0:T(8,128)(2,1)}), bf16[16,48,1536]{2,1,0:T(8,128)(2,1)}, u32[]{:S(2)}, u32[]{:S(2)}) async-start(bf16[16,48,1536]{2,1,0:T(8,128)(2,1)} %broadcast_in_dim.15), calls=%async_computation.1 | async-start | bytes 4718592 | tf_op jit(solution)/shard_map/all_to_all | solution.py:14
  122.3 12.4 %all-to-all-start.5 = ((f32[16,8,128]{2,1,0:T(8,128)}), f32[16,8,128]{2,1,0:T(8,128)S(1)}, u32[]{:S(2)}, u32[]{:S(2)}) async-start(f32[16,8,128]{2,1,0:T(8,128)} %broadcast_in_dim.31), calls=%async_computation.5 | async-start | bytes 131072 | tf_op jit(solution)/shard_map/all_to_all | solution.py:27
  134.7 79.3 %all-to-all-start.2 = ((f32[16,48,1536]{2,1,0:T(8,128)}), f32[16,48,1536]{2,1,0:T(8,128)}, u32[]{:S(2)}, u32[]{:S(2)}) async-start(f32[16,48,1536]{2,1,0:T(8,128)} %bitcast.18), calls=%async_computation.2 | async-start | bytes 9437184 | tf_op jit(solution)/shard_map/all_to_all | solution.py:21
  213.9 113.0 %all-to-all-start.3 = ((f32[16,48,1536]{2,1,0:T(8,128)}), f32[16,48,1536]{2,1,0:T(8,128)}, u32[]{:S(2)}, u32[]{:S(2)}) async-start(f32[16,48,1536]{2,1,0:T(8,128)} %bitcast.17), calls=%async_computation.3 | async-start | bytes 9437184 | tf_op jit(solution)/shard_map/all_to_all | solution.py:21
